TPU v7x, 32 devices: a whole 2x2x4 slice. The times are simulated.
32 devices in a mesh: dp: 8 (over z, x), heads: 4 (over y, core).
Axes of the slice: x: 2, y: 2, z: 4, core: 2. Of those that a mesh axis runs over, the one named last changes fastest.
Arguments:
- queries: bfloat16 [8, 2048, 1024], P(None, ('dp', 'heads')), may hold values from -6 to 6
- keys: bfloat16 [8, 2048, 512], P(None, ('dp', 'heads')), may hold values from -6 to 6
- values: bfloat16 [8, 2048, 512], P(None, ('dp', 'heads')), may hold values from -6 to 6
- lengths: int32 [8, 32], replicated, may hold values from 1 to 256, 2048 in all within a row
Outputs:
- attended: bfloat16 [8, 2048, 1024], P(None, ('dp', 'heads'))
- log_norm: float32 [8, 8, 2048], P('heads', None, 'dp')
Inputs may be any that keep to these rules, and one draw needn't show every extreme that they name: In each row the 32 lengths sum to 2048, and the longest is exactly 256.
All inputs are finite; a program needn't handle non-finite values.
Results may differ from a plain program's by a relative error of at most 0.0034.
Values may be sent and summed in bfloat16 or wider, within the bound.
A program may use at most 64 MiB of HBM per device.

v0:
```python
import functools
import math

import jax
import jax.numpy as jnp
from jax import lax
from jax.experimental import pallas as pl
from jax.experimental.pallas import tpu as pltpu
from jax.sharding import PartitionSpec as P

HEAD_SIZE = 128


def from_behind(value, axis, steps):
    count = lax.axis_size(axis)
    leading, last = (max(0, -steps), min(count, count - steps))
    return lax.ppermute(value, axis, [(source, source + steps) for source in range(leading, last)])


def doc_numbers(doc_ends, positions):
    return jnp.sum((doc_ends[:, None, :] <= positions[None, :, None]).astype(jnp.int32), axis=-1)


def per_device(queries, keys, values, lengths):
    local_q, local_k, local_v = (
        lax.all_to_all(queries, "heads", split_axis=2, concat_axis=1, tiled=True),
        lax.all_to_all(keys, "heads", split_axis=2, concat_axis=1, tiled=True),
        lax.all_to_all(values, "heads", split_axis=2, concat_axis=1, tiled=True),
    )
    row_count, tok_row, q_width = local_q.shape
    kv_heads = local_k.shape[2] // HEAD_SIZE
    per_group = q_width // (kv_heads * HEAD_SIZE)
    shards = lax.axis_size("dp")
    reach_blocks = shards // 8
    dp_index = lax.axis_index("dp")
    doc_ends = jnp.cumsum(lengths, axis=1)
    query_pos = dp_index * tok_row + jnp.arange(tok_row, dtype=jnp.int32)
    query_doc = doc_numbers(doc_ends, query_pos)
    doc_starts = jnp.max(
        jnp.where(doc_ends[:, None, :] <= query_pos[None, :, None], doc_ends[:, None, :], 0),
        axis=-1,
    )
    lowest = jnp.min(doc_starts)
    query_last = dp_index * tok_row + tok_row - 1
    query_heads = local_q.reshape(row_count, tok_row, kv_heads, per_group, HEAD_SIZE)
    score_scale = HEAD_SIZE ** (-0.5)

    def attend(state_now, key_block, value_block, anchor):
        run_max, run_sum, run_acc = state_now
        span_keys = key_block.shape[1]
        key_pos = anchor + jnp.arange(span_keys, dtype=jnp.int32)
        key_doc = doc_numbers(doc_ends, key_pos)
        visible = (
            (key_doc[:, None, :] == query_doc[:, :, None])
            & (key_pos[None, None, :] <= query_pos[None, :, None])
            & (key_pos[None, None, :] >= 0)
        )
        key_heads = key_block.reshape(row_count, span_keys, kv_heads, HEAD_SIZE)
        value_heads = value_block.reshape(row_count, span_keys, kv_heads, HEAD_SIZE)
        scores = (
            jnp.einsum(
                "rtkgd,rskd->kgrts", query_heads, key_heads, preferred_element_type=jnp.float32
            )
            * score_scale
        )
        masked = jnp.where(visible[None, None], scores, -1e30)
        new_max = jnp.maximum(run_max, jnp.max(masked, axis=-1))
        weights = jnp.where(visible[None, None], jnp.exp(masked - new_max[..., None]), 0.0)
        shrink = jnp.exp(run_max - new_max)
        run_sum = run_sum * shrink + jnp.sum(weights, axis=-1)
        partial_value = jnp.einsum(
            "kgrts,rskd->rtkgd",
            weights.astype(jnp.bfloat16),
            value_heads,
            preferred_element_type=jnp.float32,
        )
        run_acc = run_acc * jnp.transpose(shrink, (2, 3, 0, 1))[..., None] + partial_value
        return (new_max, run_sum, run_acc)

    def visit(state_now, key_block, value_block, anchor):
        key_end = anchor + key_block.shape[1] - 1
        needed = (anchor <= query_last) & (key_end >= lowest) & (key_end >= 0)
        result = lax.cond(
            needed,
            lambda carried: attend(carried, key_block, value_block, anchor),
            lambda carried: carried,
            state_now,
        )
        return result

    own_block = jnp.stack((local_k, local_v))
    shift_plan = []
    held_blocks = 1
    while 2 * held_blocks <= reach_blocks + 1:
        shift_plan.append((held_blocks, held_blocks))
        held_blocks = 2 * held_blocks
    if held_blocks < reach_blocks + 1:
        shift_plan.append((held_blocks, reach_blocks + 1 - held_blocks))
    window = own_block
    for distance, block_total in shift_plan:
        newest = window[:, :, window.shape[2] - block_total * tok_row :]
        earlier = from_behind(newest, "dp", distance)
        window = jnp.concatenate((earlier, window), axis=2)
    anchor_first = (dp_index - reach_blocks) * tok_row
    key_window = window[0]
    value_window = window[1]

    def advance(block_index, carried):
        key_block = lax.dynamic_slice_in_dim(key_window, block_index * tok_row, tok_row, 1)
        value_block = lax.dynamic_slice_in_dim(value_window, block_index * tok_row, tok_row, 1)
        return visit(carried, key_block, value_block, anchor_first + block_index * tok_row)

    initial = (
        jnp.full((kv_heads, per_group, row_count, tok_row), -1e30, jnp.float32),
        jnp.zeros((kv_heads, per_group, row_count, tok_row), jnp.float32),
        jnp.zeros((row_count, tok_row, kv_heads, per_group, HEAD_SIZE), jnp.float32),
    )
    folded = lax.fori_loop(0, reach_blocks + 1, advance, initial)
    run_max, run_sum, run_acc = folded
    scaled = run_acc / jnp.transpose(run_sum, (2, 3, 0, 1))[..., None]
    attended = scaled.astype(jnp.bfloat16).reshape(row_count, tok_row, q_width)
    spread = lax.all_to_all(attended, "heads", split_axis=1, concat_axis=2, tiled=True)
    log_norm = (run_max + jnp.log(run_sum)).reshape(kv_heads * per_group, row_count, tok_row)
    return (spread, log_norm)

MESH = pl.DeviceIdType.MESH


def fused_kernel(
    shards, q_ref, k_ref, v_ref, len_ref, out_ref, norm_ref,
    kv, qs, outs, lens, starts, columns, norms, held, inverse, stage, stage_half, k_all, v_all,
    sem_len, sem_own, recv_own, recv_x, recv_y, send_x, send_y, send_own,
    recv_out, send_out, local_out, recv_norm, send_norm, send_stage, recv_stage, sem_load,
):
    rows, tok, q_width = q_ref.shape
    kv_half = k_ref.shape[2] // 2
    q_half = q_width // 2
    kv_heads = kv_half // HEAD_SIZE
    per_group = q_half // kv_half
    docs = len_ref.shape[1]
    span = 6 * tok
    dp = lax.axis_index("dp")
    index = lax.axis_index("heads")
    y = index // 2
    core = index % 2
    has_prev = dp > 0
    has_next = dp < shards - 1

    def at(d, chip, c):
        return {"dp": d, "heads": 2 * chip + c}

    def remote(src, dst, send, recv, device):
        return pltpu.make_async_remote_copy(
            src_ref=src, dst_ref=dst, send_sem=send, recv_sem=recv,
            device_id=device, device_id_type=MESH,
        )

    def drain(ref, sem):
        pltpu.make_async_copy(ref, ref, sem).wait()

    barrier = pltpu.get_barrier_semaphore()

    def greet(device):
        pl.semaphore_signal(barrier, inc=1, device_id=device, device_id_type=MESH)

    @pl.when(has_prev)
    def _():
        greet(at(dp - 1, y, 0))
        greet(at(dp - 1, y, 1))

    greet(at(dp, 1 - y, 0))
    greet(at(dp, 1 - y, 1))
    greet(at(dp, y, 1 - core))

    def part(ref, c):
        width = ref.shape[2] // 2
        return (slice(None), pl.ds(pl.multiple_of(c * width, width), width))

    load_k = pltpu.make_async_copy(k_ref, k_all, sem_load.at[0])
    load_v = pltpu.make_async_copy(v_ref, v_all, sem_load.at[1])
    load_k.start()
    load_v.start()

    len_copy = pltpu.make_async_copy(len_ref, lens, sem_len)
    len_copy.start()
    mine = (
        pltpu.make_async_copy(q_ref.at[(slice(None),) + part(q_ref, core)], qs.at[:, core], sem_own.at[0]),
        pltpu.make_async_copy(k_ref.at[(slice(None),) + part(k_ref, core)], kv.at[:, 0, 4 + core], sem_own.at[1]),
        pltpu.make_async_copy(v_ref.at[(slice(None),) + part(v_ref, core)], kv.at[:, 1, 4 + core], sem_own.at[2]),
    )
    for copy in mine:
        copy.start()

    pl.semaphore_wait(
        barrier, 3 + 2 * has_next.astype(jnp.int32)
    )

    def send_rows(which, ref):
        def send_row(r, carry):
            @pl.when(has_next)
            def _():
                for c in (0, 1):
                    remote(
                        ref.at[(r,) + part(ref, c)], kv.at[r, which, core],
                        send_x, recv_x.at[r, which], at(dp + 1, y, c),
                    ).start()

            @pl.when(y == 0)
            def _():
                for c in (0, 1):
                    remote(
                        ref.at[(r,) + part(ref, c)], kv.at[r, which, 2 + core],
                        send_y.at[r, which], recv_y.at[r, which], at(dp, 1, c),
                    ).start()

            return carry

        lax.fori_loop(0, rows, send_row, 0)

    load_k.wait()
    send_rows(0, k_all)
    load_v.wait()

    across = jnp.logical_and(has_next, y == 1)
    onward = jnp.logical_and(has_next, y == 0)

    @pl.when(across)
    def _():
        for c in (0, 1):
            remote(
                v_all.at[(rows - 1,) + part(v_ref, c)], stage.at[core],
                send_stage.at[0], recv_stage.at[0], at(dp, 0, c),
            ).start()
            remote(
                v_all.at[rows - 2, :, pl.ds(c * kv_half, kv_half // 2)], stage_half.at[core],
                send_stage.at[1], recv_stage.at[1], at(dp, 0, c),
            ).start()

    send_rows(1, v_all)

    partner = at(dp, y, 1 - core)
    theirs = (
        remote(q_ref.at[(slice(None),) + part(q_ref, 1 - core)], qs.at[:, core], send_own.at[0], recv_own.at[0], partner),
        remote(k_ref.at[(slice(None),) + part(k_ref, 1 - core)], kv.at[:, 0, 4 + core], send_own.at[1], recv_own.at[1], partner),
        remote(v_ref.at[(slice(None),) + part(v_ref, 1 - core)], kv.at[:, 1, 4 + core], send_own.at[2], recv_own.at[2], partner),
    )
    for copy in theirs:
        copy.start()

    @pl.when(jnp.logical_not(has_prev))
    def _():
        kv[:, :, 0:2] = jnp.zeros((rows, 2, 2, tok, kv_half), kv.dtype)

        @pl.when(y == 0)
        def _():
            kv[:, :, 2:4] = jnp.zeros((rows, 2, 2, tok, kv_half), kv.dtype)

    len_copy.wait()
    base = (4 * dp + 2 * y) * tok
    upto = lax.broadcasted_iota(jnp.int32, (docs, docs), 0) <= lax.broadcasted_iota(jnp.int32, (docs, docs), 1)
    ends = jnp.dot(
        lens[...].astype(jnp.float32), upto.astype(jnp.float32),
        precision=lax.Precision.HIGHEST, preferred_element_type=jnp.float32,
    )
    query = (lax.broadcasted_iota(jnp.int32, (2 * tok, docs), 0) + base).astype(jnp.float32)
    for r in range(rows):
        row_ends = ends[r : r + 1, :]
        first = jnp.max(jnp.where(row_ends <= query, row_ends, 0.0), axis=1, keepdims=True)
        starts[r] = jnp.broadcast_to(first.astype(jnp.int32) - (base - 4 * tok), (2 * tok, HEAD_SIZE))

    for copy in mine:
        copy.wait()
    for copy in theirs:
        copy.wait_recv()

    @pl.when(onward)
    def _():
        drain(stage_half, recv_stage.at[1])
        remote(
            stage_half, kv.at[rows - 2, 1, 2:4, :, 0 : kv_half // 2], send_stage.at[1],
            recv_y.at[rows - 2, 1], at(dp + 1, 0, core),
        ).start()
        drain(stage, recv_stage.at[0])
        remote(
            stage, kv.at[rows - 1, 1, 2:4], send_stage.at[0], recv_y.at[rows - 1, 1],
            at(dp + 1, 0, core),
        ).start()

    factor = HEAD_SIZE ** (-0.5)
    power = factor / math.log(2.0)
    lane = lax.broadcasted_iota(jnp.int32, (2 * tok, HEAD_SIZE), 1)

    q_heads = kv_heads * per_group
    half = q_heads // 2
    spot = pl.ds(pl.multiple_of(y * 2 * tok, 2 * tok), 2 * tok)

    def arrived(r, which):
        @pl.when(has_prev)
        def _():
            drain(kv.at[r, which, 0:2], recv_x.at[r, which])

            relayed = y == 1
            if which == 1:
                relayed = jnp.logical_and(relayed, r < rows - 2)

                @pl.when(jnp.logical_and(y == 1, r == rows - 2))
                def _():
                    rest = slice(kv_half // 2, kv_half)
                    remote(
                        kv.at[r, which, 0:2, :, rest], kv.at[r, which, 2:4, :, rest],
                        send_y.at[r, which], recv_y.at[r, which], at(dp, 0, core),
                    ).start()

            @pl.when(relayed)
            def _():
                remote(
                    kv.at[r, which, 0:2], kv.at[r, which, 2:4],
                    send_y.at[r, which], recv_y.at[r, which], at(dp, 0, core),
                ).start()

        @pl.when(jnp.logical_or(has_prev, y == 1))
        def _():
            drain(kv.at[r, which, 2:4], recv_y.at[r, which])

    def send_norms():
        turned = columns[...].T
        norms[...] = turned[0 : q_heads * rows].reshape(q_heads, rows, 2 * tok)
        for t in (0, 1):
            own = jnp.logical_and(y == core, core == t)
            source = norms.at[t * half : (t + 1) * half]

            @pl.when(own)
            def _():
                pltpu.make_async_copy(source, norm_ref.at[:, :, spot], recv_norm.at[y]).start()

            @pl.when(jnp.logical_not(own))
            def _():
                remote(source, norm_ref.at[:, :, spot], send_norm.at[t], recv_norm.at[y], at(dp, core, t)).start()

    def score_row(r, carry):
        arrived(r, 0)
        key_at = lax.broadcasted_iota(jnp.int32, (2 * tok, span), 1)
        last = lax.broadcasted_iota(jnp.int32, (2 * tok, span), 0) + 4 * tok
        first = starts[r][:, 0:1]
        visible = (key_at >= first) & (key_at <= last)
        found = columns[...]
        for j in range(q_heads):
            head = j // per_group
            at_kv = slice(head * HEAD_SIZE, (head + 1) * HEAD_SIZE)
            at_q = slice(j * HEAD_SIZE, (j + 1) * HEAD_SIZE)
            keys = kv[r, 0, :, :, at_kv].reshape(span, HEAD_SIZE)
            query_rows = qs[r, :, :, at_q].reshape(2 * tok, HEAD_SIZE)
            products = lax.dot_general(
                query_rows, keys, (((1,), (1,)), ((), ())),
                preferred_element_type=jnp.float32,
            )
            masked = jnp.where(visible, products, -1e30)
            top = jnp.max(masked, axis=1, keepdims=True)
            weights = jnp.exp2((masked - top) * power)
            total = jnp.sum(weights, axis=1, keepdims=True)
            held[r, j] = weights.astype(jnp.bfloat16)
            inverse[r, j] = jnp.broadcast_to(1.0 / total, (2 * tok, HEAD_SIZE))
            found = jnp.where(lane == j * rows + r, top * factor + jnp.log(total), found)
        columns[...] = found
        return carry

    def mix_row(r, carry):
        arrived(r, 1)
        for j in range(q_heads):
            head = j // per_group
            at_kv = slice(head * HEAD_SIZE, (head + 1) * HEAD_SIZE)
            at_q = slice(j * HEAD_SIZE, (j + 1) * HEAD_SIZE)
            vals = kv[r, 1, :, :, at_kv].reshape(span, HEAD_SIZE)
            mixed = jnp.dot(held[r, j], vals, preferred_element_type=jnp.float32)
            outs[r, :, :, at_q] = (
                (mixed * inverse[r, j]).astype(jnp.bfloat16).reshape(2, tok, HEAD_SIZE)
            )
        place = (r, slice(None), pl.ds(pl.multiple_of(core * q_half, q_half), q_half))
        remote(
            outs.at[r, 1 - core], out_ref.at[place], send_out, recv_out, partner
        ).start()
        pltpu.make_async_copy(outs.at[r, core], out_ref.at[place], local_out).start()
        return carry

    columns[...] = jnp.zeros(columns.shape, jnp.float32)
    lax.fori_loop(0, rows, score_row, 0)
    send_norms()
    lax.fori_loop(0, rows, mix_row, 0)

    for copy in theirs:
        copy.wait_send()

    @pl.when(has_next)
    def _():
        drain(kv.at[:, :, 0:2], send_x)

    for which in (0, 1):
        for r in range(rows):
            sent = jnp.logical_or(has_prev, y == 0)
            if which == 1 and r >= rows - 2:
                sent = y == 0
            if which == 1 and r == rows - 2:
                @pl.when(jnp.logical_and(has_prev, y == 1))
                def _():
                    drain(kv.at[r, which, 2:4, :, 0 : kv_half // 2], send_y.at[r, which])

            @pl.when(sent)
            def _():
                drain(kv.at[r, which, 2:4], send_y.at[r, which])

    @pl.when(has_next)
    def _():
        drain(stage, send_stage.at[0])
        drain(stage_half, send_stage.at[1])

    drain(outs.at[:, 0], local_out)
    drain(outs.at[:, 0], send_out)
    drain(outs.at[:, 0], recv_out)
    for t in (0, 1):
        @pl.when(jnp.logical_not(jnp.logical_and(y == core, core == t)))
        def _():
            drain(norms.at[0:half], send_norm.at[t])
    for t in (0, 1):
        drain(norms.at[0:half], recv_norm.at[t])


def store_kernel(out_ref, norm_ref, out_to, norm_to, sems):
    rows = out_ref.shape[0]
    copies = [pltpu.make_async_copy(norm_ref, norm_to, sems.at[rows])]
    for r in range(rows):
        copies.append(pltpu.make_async_copy(out_ref.at[r], out_to.at[r], sems.at[r]))
    for copy in copies:
        copy.start()
    for copy in copies:
        copy.wait()


def store(attended, log_norm):
    return pl.pallas_call(
        store_kernel,
        out_shape=(
            pltpu.HBM(attended.shape, attended.dtype),
            pltpu.HBM(log_norm.shape, log_norm.dtype),
        ),
        in_specs=[pl.BlockSpec(memory_space=pl.ANY)] * 2,
        out_specs=(pl.BlockSpec(memory_space=pl.ANY),) * 2,
        scratch_shapes=[pltpu.SemaphoreType.DMA((attended.shape[0] + 1,))],
    )(*(pltpu.with_memory_space_constraint(a, pltpu.VMEM) for a in (attended, log_norm)))


def fused(queries, keys, values, lengths):
    rows, tok, q_width = queries.shape
    kv_width = keys.shape[2]
    heads = lax.axis_size("heads")
    q_heads = q_width // HEAD_SIZE
    dma = pltpu.SemaphoreType.DMA
    results = pl.pallas_call(
        functools.partial(fused_kernel, lax.axis_size("dp")),
        out_shape=(
            pltpu.VMEM((rows, tok, q_width), jnp.bfloat16),
            pltpu.VMEM((q_heads // heads, rows, heads * tok), jnp.float32),
        ),
        in_specs=[pl.BlockSpec(memory_space=pltpu.HBM)] * 4,
        out_specs=(pl.BlockSpec(memory_space=pl.ANY),) * 2,
        scratch_shapes=[
            pltpu.VMEM((rows, 2, 6, tok, kv_width // 2), jnp.bfloat16),
            pltpu.VMEM((rows, 2, tok, q_width // 2), jnp.bfloat16),
            pltpu.VMEM((rows, 2, tok, q_width // 2), jnp.bfloat16),
            pltpu.VMEM(lengths.shape, jnp.int32),
            pltpu.VMEM((rows, 2 * tok, HEAD_SIZE), jnp.int32),
            pltpu.VMEM((2 * tok, HEAD_SIZE), jnp.float32),
            pltpu.VMEM((q_heads // 2, rows, 2 * tok), jnp.float32),
            pltpu.VMEM((rows, q_heads // 2, 2 * tok, 6 * tok), jnp.bfloat16),
            pltpu.VMEM((rows, q_heads // 2, 2 * tok, HEAD_SIZE), jnp.float32),
            pltpu.VMEM((2, tok, kv_width // 2), jnp.bfloat16),
            pltpu.VMEM((2, tok, kv_width // 4), jnp.bfloat16),
            pltpu.VMEM(keys.shape, jnp.bfloat16),
            pltpu.VMEM(values.shape, jnp.bfloat16),
            dma, dma((3,)), dma((3,)), dma((rows, 2)), dma((rows, 2)),
            dma, dma((rows, 2)), dma((3,)), dma, dma, dma, dma((2,)), dma((2,)), dma((2,)), dma((2,)), dma((2,)),
        ],
        compiler_params=pltpu.CompilerParams(
            collective_id=0, has_side_effects=True, vmem_limit_bytes=48 * 1024 * 1024
        ),
    )(*(pltpu.with_memory_space_constraint(a, pltpu.HBM) for a in (queries, keys, values, lengths)))
    return store(*results)


def dispatch(queries, keys, values, lengths):
    heads, shards = lax.axis_size("heads"), lax.axis_size("dp")
    tok = queries.shape[1]
    suited = (
        heads == 4
        and shards // 8 == 1
        and shards > 2
        and 2 * tok == HEAD_SIZE
        and keys.shape[2] == heads * HEAD_SIZE
        and queries.shape[2] * queries.shape[0] <= 2 * HEAD_SIZE * HEAD_SIZE
    )
    return (fused if suited else per_device)(queries, keys, values, lengths)


def solution(mesh):
    in_specs = (
        P(None, ("dp", "heads"), None),
        P(None, ("dp", "heads"), None),
        P(None, ("dp", "heads"), None),
        P(),
    )
    out_specs = (P(None, ("dp", "heads"), None), P("heads", None, "dp"))
    return jax.shard_map(
        dispatch, mesh=mesh, in_specs=in_specs, out_specs=out_specs, check_vma=False
    )
```

profile of v0, /device:TPU:25, one launch (start us, length us, event | category | flops | bytes accessed | tf_op | source)
XLA Modules:
  0.0 32.9 jit_solution(9407530104748942195)
XLA Ops:
  0.6 31.3 %shard_map.59 = (bf16[8,64,1024]{2,1,0:T(8,128)(2,1)S(1)}, f32[2,8,256]{2,1,0:T(8,128)S(1)}) custom-call(bf16[8,64,1024]{2,1,0:T(8,128)(2,1)} %q_ref.1, bf16[8,64,512]{2,1,0:T(8,128)(2,1)} %k_ref.1, bf16[8,64,512]{2,1,0:T(8,128)(2,1)} %v_ref.1, s32[8,32]{1,0:T(8,128)} %len_ref.1), custom_call_target="tpu_custom_call" | custom-call | tf_op jit(solution)/shard_map/pallas_call | solution.py:457
  31.9 1.0 %shard_map.60 = (bf16[8,64,1024]{2,1,0:T(8,128)(2,1)}, f32[2,8,256]{2,1,0:T(8,128)}) custom-call(bf16[8,64,1024]{2,1,0:T(8,128)(2,1)S(1)} %get-tuple-element.4.out_ref, f32[2,8,256]{2,1,0:T(8,128)S(1)} %get-tuple-element.5.norm_ref), custom_call_target="tpu_custom_call" | custom-call | tf_op jit(solution)/shard_map/pallas_call | solution.py:439
where the time goes:
time: 33.1 us; the launch traced here: 32.9 us
  Pallas kernels  32.3 us (98%)
  between operations  0.64 us (2%)
    pallas_call x1, Pallas kernels, fused(): pl.pallas_call(functools.partial(fused_kernel, lax.axis_size('dp')), out_...  31.3 us
    pallas_call x1, Pallas kernels, store(): pl.pallas_call(store_kernel, out_shape=(pltpu.HBM(attended.shape, attende...  1.04 us

commit v1 on v0

--- a/solution.py
+++ b/solution.py
@@ -129,8 +129,7 @@
 def fused_kernel(
     shards, q_ref, k_ref, v_ref, len_ref, out_ref, norm_ref,
     kv, qs, outs, lens, starts, columns, norms, held, inverse, stage, stage_half, k_all, v_all,
-    sem_len, sem_own, recv_own, recv_x, recv_y, send_x, send_y, send_own,
-    recv_out, send_out, local_out, recv_norm, send_norm, send_stage, recv_stage, sem_load,
+    sem_len, sem_own, recv_own, recv_x, recv_y, sends, recv_out, recv_norm, recv_stage, sem_load,
 ):
     rows, tok, q_width = q_ref.shape
     kv_half = k_ref.shape[2] // 2
@@ -184,9 +183,9 @@
     len_copy = pltpu.make_async_copy(len_ref, lens, sem_len)
     len_copy.start()
     mine = (
-        pltpu.make_async_copy(q_ref.at[(slice(None),) + part(q_ref, core)], qs.at[:, core], sem_own.at[0]),
-        pltpu.make_async_copy(k_ref.at[(slice(None),) + part(k_ref, core)], kv.at[:, 0, 4 + core], sem_own.at[1]),
-        pltpu.make_async_copy(v_ref.at[(slice(None),) + part(v_ref, core)], kv.at[:, 1, 4 + core], sem_own.at[2]),
+        pltpu.make_async_copy(q_ref.at[(slice(None),) + part(q_ref, core)], qs.at[:, core], sem_own),
+        pltpu.make_async_copy(k_ref.at[(slice(None),) + part(k_ref, core)], kv.at[:, 0, 4 + core], sem_own),
+        pltpu.make_async_copy(v_ref.at[(slice(None),) + part(v_ref, core)], kv.at[:, 1, 4 + core], sem_own),
     )
     for copy in mine:
         copy.start()
@@ -194,6 +193,11 @@
     pl.semaphore_wait(
         barrier, 3 + 2 * has_next.astype(jnp.int32)
     )
+
+    def group(r, which):
+        if which == 0:
+            return 2 * r // rows
+        return 2 + (2 * r // rows) + jnp.maximum(r - (rows - 3), 0)
 
     def send_rows(which, ref):
         def send_row(r, carry):
@@ -202,7 +206,7 @@
                 for c in (0, 1):
                     remote(
                         ref.at[(r,) + part(ref, c)], kv.at[r, which, core],
-                        send_x, recv_x.at[r, which], at(dp + 1, y, c),
+                        sends, recv_x.at[r, which], at(dp + 1, y, c),
                     ).start()
 
             @pl.when(y == 0)
@@ -210,7 +214,7 @@
                 for c in (0, 1):
                     remote(
                         ref.at[(r,) + part(ref, c)], kv.at[r, which, 2 + core],
-                        send_y.at[r, which], recv_y.at[r, which], at(dp, 1, c),
+                        sends, recv_y.at[group(r, which)], at(dp, 1, c),
                     ).start()
 
             return carry
@@ -229,20 +233,20 @@
         for c in (0, 1):
             remote(
                 v_all.at[(rows - 1,) + part(v_ref, c)], stage.at[core],
-                send_stage.at[0], recv_stage.at[0], at(dp, 0, c),
+                sends, recv_stage.at[0], at(dp, 0, c),
             ).start()
             remote(
                 v_all.at[rows - 2, :, pl.ds(c * kv_half, kv_half // 2)], stage_half.at[core],
-                send_stage.at[1], recv_stage.at[1], at(dp, 0, c),
+                sends, recv_stage.at[1], at(dp, 0, c),
             ).start()
 
     send_rows(1, v_all)
 
     partner = at(dp, y, 1 - core)
     theirs = (
-        remote(q_ref.at[(slice(None),) + part(q_ref, 1 - core)], qs.at[:, core], send_own.at[0], recv_own.at[0], partner),
-        remote(k_ref.at[(slice(None),) + part(k_ref, 1 - core)], kv.at[:, 0, 4 + core], send_own.at[1], recv_own.at[1], partner),
-        remote(v_ref.at[(slice(None),) + part(v_ref, 1 - core)], kv.at[:, 1, 4 + core], send_own.at[2], recv_own.at[2], partner),
+        remote(q_ref.at[(slice(None),) + part(q_ref, 1 - core)], qs.at[:, core], sends, recv_own, partner),
+        remote(k_ref.at[(slice(None),) + part(k_ref, 1 - core)], kv.at[:, 0, 4 + core], sends, recv_own, partner),
+        remote(v_ref.at[(slice(None),) + part(v_ref, 1 - core)], kv.at[:, 1, 4 + core], sends, recv_own, partner),
     )
     for copy in theirs:
         copy.start()
@@ -268,21 +272,17 @@
         first = jnp.max(jnp.where(row_ends <= query, row_ends, 0.0), axis=1, keepdims=True)
         starts[r] = jnp.broadcast_to(first.astype(jnp.int32) - (base - 4 * tok), (2 * tok, HEAD_SIZE))
 
-    for copy in mine:
-        copy.wait()
-    for copy in theirs:
-        copy.wait_recv()
 
     @pl.when(onward)
     def _():
         drain(stage_half, recv_stage.at[1])
         remote(
-            stage_half, kv.at[rows - 2, 1, 2:4, :, 0 : kv_half // 2], send_stage.at[1],
-            recv_y.at[rows - 2, 1], at(dp + 1, 0, core),
+            stage_half, kv.at[rows - 2, 1, 2:4, :, 0 : kv_half // 2], sends,
+            recv_y.at[group(rows - 2, 1)], at(dp + 1, 0, core),
         ).start()
         drain(stage, recv_stage.at[0])
         remote(
-            stage, kv.at[rows - 1, 1, 2:4], send_stage.at[0], recv_y.at[rows - 1, 1],
+            stage, kv.at[rows - 1, 1, 2:4], sends, recv_y.at[group(rows - 1, 1)],
             at(dp + 1, 0, core),
         ).start()
 
@@ -294,11 +294,10 @@
     half = q_heads // 2
     spot = pl.ds(pl.multiple_of(y * 2 * tok, 2 * tok), 2 * tok)
 
-    def arrived(r, which):
+    def take(r, which):
         @pl.when(has_prev)
         def _():
             drain(kv.at[r, which, 0:2], recv_x.at[r, which])
-
             relayed = y == 1
             if which == 1:
                 relayed = jnp.logical_and(relayed, r < rows - 2)
@@ -308,19 +307,20 @@
                     rest = slice(kv_half // 2, kv_half)
                     remote(
                         kv.at[r, which, 0:2, :, rest], kv.at[r, which, 2:4, :, rest],
-                        send_y.at[r, which], recv_y.at[r, which], at(dp, 0, core),
+                        sends, recv_y.at[group(r, which)], at(dp, 0, core),
                     ).start()
 
             @pl.when(relayed)
             def _():
                 remote(
                     kv.at[r, which, 0:2], kv.at[r, which, 2:4],
-                    send_y.at[r, which], recv_y.at[r, which], at(dp, 0, core),
+                    sends, recv_y.at[group(r, which)], at(dp, 0, core),
                 ).start()
 
+    def gathered(first, count, which):
         @pl.when(jnp.logical_or(has_prev, y == 1))
         def _():
-            drain(kv.at[r, which, 2:4], recv_y.at[r, which])
+            drain(kv.at[first : first + count, which, 2:4], recv_y.at[group(first, which)])
 
     def send_norms():
         turned = columns[...].T
@@ -331,14 +331,13 @@
 
             @pl.when(own)
             def _():
-                pltpu.make_async_copy(source, norm_ref.at[:, :, spot], recv_norm.at[y]).start()
+                pltpu.make_async_copy(source, norm_ref.at[:, :, spot], recv_norm).start()
 
             @pl.when(jnp.logical_not(own))
             def _():
-                remote(source, norm_ref.at[:, :, spot], send_norm.at[t], recv_norm.at[y], at(dp, core, t)).start()
-
-    def score_row(r, carry):
-        arrived(r, 0)
+                remote(source, norm_ref.at[:, :, spot], sends, recv_norm, at(dp, core, t)).start()
+
+    def score_row(r):
         key_at = lax.broadcasted_iota(jnp.int32, (2 * tok, span), 1)
         last = lax.broadcasted_iota(jnp.int32, (2 * tok, span), 0) + 4 * tok
         first = starts[r][:, 0:1]
@@ -362,10 +361,8 @@
             inverse[r, j] = jnp.broadcast_to(1.0 / total, (2 * tok, HEAD_SIZE))
             found = jnp.where(lane == j * rows + r, top * factor + jnp.log(total), found)
         columns[...] = found
-        return carry
-
-    def mix_row(r, carry):
-        arrived(r, 1)
+
+    def mix_row(r):
         for j in range(q_heads):
             head = j // per_group
             at_kv = slice(head * HEAD_SIZE, (head + 1) * HEAD_SIZE)
@@ -377,58 +374,83 @@
             )
         place = (r, slice(None), pl.ds(pl.multiple_of(core * q_half, q_half), q_half))
         remote(
-            outs.at[r, 1 - core], out_ref.at[place], send_out, recv_out, partner
+            outs.at[r, 1 - core], out_ref.at[place], sends, recv_out, partner
         ).start()
-        pltpu.make_async_copy(outs.at[r, core], out_ref.at[place], local_out).start()
-        return carry
+        pltpu.make_async_copy(outs.at[r, core], out_ref.at[place], recv_out).start()
+
+    part_rows = rows // 2
+
+    def each(body):
+        def step(i, carry):
+            body(i)
+            return carry
+
+        lax.fori_loop(0, part_rows, step, 0)
+
+    def first_scores(i):
+        take(part_rows + i, 0)
+        score_row(i)
+
+    def later_scores(i):
+        take(i, 1)
+        score_row(part_rows + i)
+
+    def first_mixes(i):
+        take(part_rows + i, 1)
+        mix_row(i)
 
     columns[...] = jnp.zeros(columns.shape, jnp.float32)
-    lax.fori_loop(0, rows, score_row, 0)
+    each(lambda i: take(i, 0))
+    drain(qs, sem_own)
+    drain(qs, recv_own)
+    gathered(0, part_rows, 0)
+    each(first_scores)
+    gathered(part_rows, part_rows, 0)
+    each(later_scores)
     send_norms()
-    lax.fori_loop(0, rows, mix_row, 0)
-
-    for copy in theirs:
-        copy.wait_send()
+    gathered(0, part_rows, 1)
+    each(first_mixes)
+    gathered(part_rows, part_rows - 2, 1)
+    for r in range(part_rows, rows - 2):
+        mix_row(r)
+    for r in (rows - 2, rows - 1):
+        gathered(r, 1, 1)
+        mix_row(r)
+
+    drain(qs, sends)
 
     @pl.when(has_next)
     def _():
-        drain(kv.at[:, :, 0:2], send_x)
-
-    for which in (0, 1):
-        for r in range(rows):
-            sent = jnp.logical_or(has_prev, y == 0)
-            if which == 1 and r >= rows - 2:
-                sent = y == 0
-            if which == 1 and r == rows - 2:
-                @pl.when(jnp.logical_and(has_prev, y == 1))
-                def _():
-                    drain(kv.at[r, which, 2:4, :, 0 : kv_half // 2], send_y.at[r, which])
-
-            @pl.when(sent)
-            def _():
-                drain(kv.at[r, which, 2:4], send_y.at[r, which])
-
-    @pl.when(has_next)
-    def _():
-        drain(stage, send_stage.at[0])
-        drain(stage_half, send_stage.at[1])
-
-    drain(outs.at[:, 0], local_out)
-    drain(outs.at[:, 0], send_out)
-    drain(outs.at[:, 0], recv_out)
-    for t in (0, 1):
-        @pl.when(jnp.logical_not(jnp.logical_and(y == core, core == t)))
-        def _():
-            drain(norms.at[0:half], send_norm.at[t])
-    for t in (0, 1):
-        drain(norms.at[0:half], recv_norm.at[t])
+        drain(kv.at[:, :, 0:2], sends)
+        drain(stage, sends)
+        drain(stage_half, sends)
+
+    @pl.when(y == 0)
+    def _():
+        drain(kv.at[:, :, 2:4], sends)
+
+    @pl.when(jnp.logical_and(has_prev, y == 1))
+    def _():
+        drain(kv.at[:, 0, 2:4], sends)
+        drain(kv.at[0 : rows - 2, 1, 2:4], sends)
+        drain(kv.at[0, 1, 2:4, :, 0 : kv_half // 2], sends)
+
+    drain(outs.at[:, 0], sends)
+    drain(norms.at[0:half], sends)
+
+    @pl.when(y != core)
+    def _():
+        drain(norms.at[0:half], sends)
+
+    drain(outs, recv_out)
+    drain(norms, recv_norm)
 
 
 def store_kernel(out_ref, norm_ref, out_to, norm_to, sems):
-    rows = out_ref.shape[0]
-    copies = [pltpu.make_async_copy(norm_ref, norm_to, sems.at[rows])]
-    for r in range(rows):
-        copies.append(pltpu.make_async_copy(out_ref.at[r], out_to.at[r], sems.at[r]))
+    copies = [
+        pltpu.make_async_copy(norm_ref, norm_to, sems.at[1]),
+        pltpu.make_async_copy(out_ref, out_to, sems.at[0]),
+    ]
     for copy in copies:
         copy.start()
     for copy in copies:
@@ -444,7 +466,7 @@
         ),
         in_specs=[pl.BlockSpec(memory_space=pl.ANY)] * 2,
         out_specs=(pl.BlockSpec(memory_space=pl.ANY),) * 2,
-        scratch_shapes=[pltpu.SemaphoreType.DMA((attended.shape[0] + 1,))],
+        scratch_shapes=[pltpu.SemaphoreType.DMA((2,))],
     )(*(pltpu.with_memory_space_constraint(a, pltpu.VMEM) for a in (attended, log_norm)))
 
 
@@ -476,8 +498,7 @@
             pltpu.VMEM((2, tok, kv_width // 4), jnp.bfloat16),
             pltpu.VMEM(keys.shape, jnp.bfloat16),
             pltpu.VMEM(values.shape, jnp.bfloat16),
-            dma, dma((3,)), dma((3,)), dma((rows, 2)), dma((rows, 2)),
-            dma, dma((rows, 2)), dma((3,)), dma, dma, dma, dma((2,)), dma((2,)), dma((2,)), dma((2,)), dma((2,)),
+            dma, dma, dma, dma((rows, 2)), dma((6,)), dma, dma, dma, dma((2,)), dma((2,)),
         ],
         compiler_params=pltpu.CompilerParams(
             collective_id=0, has_side_effects=True, vmem_limit_bytes=48 * 1024 * 1024
@@ -495,6 +516,8 @@
         and shards > 2
         and 2 * tok == HEAD_SIZE
         and keys.shape[2] == heads * HEAD_SIZE
+        and queries.shape[0] % 2 == 0
+        and queries.shape[0] >= 8
         and queries.shape[2] * queries.shape[0] <= 2 * HEAD_SIZE * HEAD_SIZE
     )
     return (fused if suited else per_device)(queries, keys, values, lengths)

time: 33.1 us -> 32.7 us (0.988)
  Pallas kernels: 32.3 us -> 31.9 us
    pallas_call x1, Pallas kernels: 31.3 us -> 30.9 us  [fused(): pl.pallas_call(functools.partial(fused_kernel, lax.axis_size('dp')), out_...]
where the time goes in v1:
time: 32.7 us; the launch traced here: 32.5 us
  Pallas kernels  31.9 us (98%)
  between operations  0.64 us (2%)
    pallas_call x1, Pallas kernels, fused(): pl.pallas_call(functools.partial(fused_kernel, lax.axis_size('dp')), out_...  30.9 us
    pallas_call x1, Pallas kernels, store(): pl.pallas_call(store_kernel, out_shape=(pltpu.HBM(attended.shape, attende...  0.99 us

profile of v1, /device:TPU:25, one launch (start us, length us, event | category | flops | bytes accessed | tf_op | source)
XLA Modules:
  0.0 32.5 jit_solution(12075906083998457144)
XLA Ops:
  0.6 30.9 %shard_map.59 = (bf16[8,64,1024]{2,1,0:T(8,128)(2,1)S(1)}, f32[2,8,256]{2,1,0:T(8,128)S(1)}) custom-call(bf16[8,64,1024]{2,1,0:T(8,128)(2,1)} %q_ref.1, bf16[8,64,512]{2,1,0:T(8,128)(2,1)} %k_ref.1, bf16[8,64,512]{2,1,0:T(8,128)(2,1)} %v_ref.1, s32[8,32]{1,0:T(8,128)} %len_ref.1), custom_call_target="tpu_custom_call" | custom-call | tf_op jit(solution)/shard_map/pallas_call | solution.py:479
  31.5 1.0 %shard_map.60 = (bf16[8,64,1024]{2,1,0:T(8,128)(2,1)}, f32[2,8,256]{2,1,0:T(8,128)}) custom-call(bf16[8,64,1024]{2,1,0:T(8,128)(2,1)S(1)} %get-tuple-element.4.out_ref, f32[2,8,256]{2,1,0:T(8,128)S(1)} %get-tuple-element.5.norm_ref), custom_call_target="tpu_custom_call" | custom-call | tf_op jit(solution)/shard_map/pallas_call | solution.py:461

commit v2 on v1

--- a/solution.py
+++ b/solution.py
@@ -128,8 +128,8 @@
 
 def fused_kernel(
     shards, q_ref, k_ref, v_ref, len_ref, out_ref, norm_ref,
-    kv, qs, outs, lens, starts, columns, norms, held, inverse, stage, stage_half, k_all, v_all,
-    sem_len, sem_own, recv_own, recv_x, recv_y, sends, recv_out, recv_norm, recv_stage, sem_load,
+    kv, qs, outs, lens, starts, columns, norms, held, inverse, stage, stage_late, detour, k_all, v_all,
+    sem_len, sem_own, recv_own, recv_x, recv_y, sends, recv_out, recv_norm, recv_stage, recv_detour, sem_load, landed,
 ):
     rows, tok, q_width = q_ref.shape
     kv_half = k_ref.shape[2] // 2
@@ -144,6 +144,15 @@
     core = index % 2
     has_prev = dp > 0
     has_next = dp < shards - 1
+    odd = dp % 2 == 1
+    even = dp % 2 == 0
+    around = rows // 4
+    lands = jnp.logical_and(y == 0, jnp.logical_and(even, has_prev))
+    detours = jnp.logical_and(y == 0, jnp.logical_and(odd, has_next))
+    passes = jnp.logical_and(y == 0, dp == 0)
+    sent_round = jnp.where(detours, around, 0)
+    landings = range(2, shards, 2)
+    half_head = kv_half // 2
 
     def at(d, chip, c):
         return {"dp": d, "heads": 2 * chip + c}
@@ -170,6 +179,13 @@
     greet(at(dp, 1 - y, 0))
     greet(at(dp, 1 - y, 1))
     greet(at(dp, y, 1 - core))
+
+    @pl.when(passes)
+    def _():
+        for d in landings:
+            greet(at(d - 1, 0, core))
+            greet(at(d, 0, 0))
+            greet(at(d, 0, 1))
 
     def part(ref, c):
         width = ref.shape[2] // 2
@@ -191,17 +207,27 @@
         copy.start()
 
     pl.semaphore_wait(
-        barrier, 3 + 2 * has_next.astype(jnp.int32)
-    )
+        barrier,
+        3 + 2 * has_next.astype(jnp.int32) + detours.astype(jnp.int32) + 2 * lands.astype(jnp.int32),
+    )
+
+    @pl.when(lands)
+    def _():
+        for c in (0, 1):
+            pl.semaphore_signal(landed, inc=1, device_id=at(0, 0, c), device_id_type=MESH)
 
     def group(r, which):
         if which == 0:
             return 2 * r // rows
-        return 2 + (2 * r // rows) + jnp.maximum(r - (rows - 3), 0)
+        return 2 + jnp.maximum(r - rows // 2 + 1, 0)
 
     def send_rows(which, ref):
         def send_row(r, carry):
-            @pl.when(has_next)
+            straight = has_next
+            if which == 1:
+                straight = jnp.logical_and(has_next, r < rows - sent_round)
+
+            @pl.when(straight)
             def _():
                 for c in (0, 1):
                     remote(
@@ -235,12 +261,28 @@
                 v_all.at[(rows - 1,) + part(v_ref, c)], stage.at[core],
                 sends, recv_stage.at[0], at(dp, 0, c),
             ).start()
-            remote(
-                v_all.at[rows - 2, :, pl.ds(c * kv_half, kv_half // 2)], stage_half.at[core],
-                sends, recv_stage.at[1], at(dp, 0, c),
-            ).start()
+
+            def late(skip):
+                width = slice(skip * half_head, (skip + 1) * half_head)
+                remote(
+                    v_all.at[rows - 2, :, pl.ds(c * kv_half + skip * half_head, half_head)],
+                    stage_late.at[core, :, width], sends, recv_stage.at[1], at(dp, 0, c),
+                ).start()
+
+            late(0)
+
+            @pl.when(odd)
+            def _():
+                late(1)
 
     send_rows(1, v_all)
+
+    @pl.when(detours)
+    def _():
+        slot = (dp - 1) // 2
+        remote(
+            v_all.at[rows - around : rows], detour.at[slot], sends, recv_detour.at[slot], at(0, 0, core)
+        ).start()
 
     partner = at(dp, y, 1 - core)
     theirs = (
@@ -275,16 +317,39 @@
 
     @pl.when(onward)
     def _():
-        drain(stage_half, recv_stage.at[1])
-        remote(
-            stage_half, kv.at[rows - 2, 1, 2:4, :, 0 : kv_half // 2], sends,
-            recv_y.at[group(rows - 2, 1)], at(dp + 1, 0, core),
-        ).start()
+        @pl.when(odd)
+        def _():
+            drain(stage_late, recv_stage.at[1])
+            remote(
+                stage_late, kv.at[rows - 2, 1, 2:4], sends, recv_y.at[group(rows - 2, 1)],
+                at(dp + 1, 0, core),
+            ).start()
+
+        @pl.when(even)
+        def _():
+            drain(stage_late.at[:, :, 0:half_head], recv_stage.at[1])
+            remote(
+                stage_late.at[:, :, 0:half_head], kv.at[rows - 2, 1, 2:4, :, 0:half_head], sends,
+                recv_y.at[group(rows - 2, 1)], at(dp + 1, 0, core),
+            ).start()
+
         drain(stage, recv_stage.at[0])
         remote(
             stage, kv.at[rows - 1, 1, 2:4], sends, recv_y.at[group(rows - 1, 1)],
             at(dp + 1, 0, core),
         ).start()
+
+    def pass_on():
+        pl.semaphore_wait(landed, 2 * len(landings))
+        for slot, d in enumerate(landings):
+            drain(detour.at[slot], recv_detour.at[slot])
+            for i in range(around):
+                for c in (0, 1):
+                    remote(
+                        detour.at[slot, i, :, c * kv_half : (c + 1) * kv_half],
+                        kv.at[rows - around + i, 1, core], sends,
+                        recv_x.at[rows - around + i, 1], at(d, 0, c),
+                    ).start()
 
     factor = HEAD_SIZE ** (-0.5)
     power = factor / math.log(2.0)
@@ -302,9 +367,9 @@
             if which == 1:
                 relayed = jnp.logical_and(relayed, r < rows - 2)
 
-                @pl.when(jnp.logical_and(y == 1, r == rows - 2))
+                @pl.when(jnp.logical_and(jnp.logical_and(y == 1, odd), r == rows - 2))
                 def _():
-                    rest = slice(kv_half // 2, kv_half)
+                    rest = slice(half_head, kv_half)
                     remote(
                         kv.at[r, which, 0:2, :, rest], kv.at[r, which, 2:4, :, rest],
                         sends, recv_y.at[group(r, which)], at(dp, 0, core),
@@ -320,7 +385,7 @@
     def gathered(first, count, which):
         @pl.when(jnp.logical_or(has_prev, y == 1))
         def _():
-            drain(kv.at[first : first + count, which, 2:4], recv_y.at[group(first, which)])
+            drain(kv.at[pl.ds(first, count), which, 2:4], recv_y.at[group(first, which)])
 
     def send_norms():
         turned = columns[...].T
@@ -362,21 +427,35 @@
             found = jnp.where(lane == j * rows + r, top * factor + jnp.log(total), found)
         columns[...] = found
 
-    def mix_row(r):
+    def mix(r, rows_of, place):
         for j in range(q_heads):
             head = j // per_group
             at_kv = slice(head * HEAD_SIZE, (head + 1) * HEAD_SIZE)
             at_q = slice(j * HEAD_SIZE, (j + 1) * HEAD_SIZE)
             vals = kv[r, 1, :, :, at_kv].reshape(span, HEAD_SIZE)
-            mixed = jnp.dot(held[r, j], vals, preferred_element_type=jnp.float32)
-            outs[r, :, :, at_q] = (
-                (mixed * inverse[r, j]).astype(jnp.bfloat16).reshape(2, tok, HEAD_SIZE)
-            )
-        place = (r, slice(None), pl.ds(pl.multiple_of(core * q_half, q_half), q_half))
+            mixed = jnp.dot(held[r, j, rows_of], vals, preferred_element_type=jnp.float32)
+            result = (mixed * inverse[r, j, rows_of]).astype(jnp.bfloat16)
+            outs[r, place, :, at_q] = result.reshape(-1, tok, HEAD_SIZE) if place == slice(None) else result
+
+    columns_of = pl.ds(pl.multiple_of(core * q_half, q_half), q_half)
+
+    def send_out(r):
         remote(
-            outs.at[r, 1 - core], out_ref.at[place], sends, recv_out, partner
+            outs.at[r, 1 - core], out_ref.at[r, :, columns_of], sends, recv_out, partner
         ).start()
-        pltpu.make_async_copy(outs.at[r, core], out_ref.at[place], recv_out).start()
+
+    def keep_out(r):
+        pltpu.make_async_copy(outs.at[r, core], out_ref.at[r, :, columns_of], recv_out).start()
+
+    def mix_row(r):
+        mix(r, slice(None), slice(None))
+        send_out(r)
+        keep_out(r)
+
+    def mix_split(r):
+        for c, finish in ((1 - core, send_out), (core, keep_out)):
+            mix(r, pl.ds(pl.multiple_of(c * tok, tok), tok), c)
+            finish(r)
 
     part_rows = rows // 2
 
@@ -401,6 +480,7 @@
 
     columns[...] = jnp.zeros(columns.shape, jnp.float32)
     each(lambda i: take(i, 0))
+    pl.when(passes)(pass_on)
     drain(qs, sem_own)
     drain(qs, recv_own)
     gathered(0, part_rows, 0)
@@ -410,12 +490,12 @@
     send_norms()
     gathered(0, part_rows, 1)
     each(first_mixes)
-    gathered(part_rows, part_rows - 2, 1)
-    for r in range(part_rows, rows - 2):
-        mix_row(r)
-    for r in (rows - 2, rows - 1):
+    late = even.astype(jnp.int32)
+    for r in [*range(part_rows, rows - 3), rows - 3 + late, rows - 1]:
         gathered(r, 1, 1)
         mix_row(r)
+    gathered(rows - 2 - late, 1, 1)
+    mix_split(rows - 2 - late)
 
     drain(qs, sends)
 
@@ -423,7 +503,11 @@
     def _():
         drain(kv.at[:, :, 0:2], sends)
         drain(stage, sends)
-        drain(stage_half, sends)
+        drain(stage_late.at[:, :, 0:half_head], sends)
+
+        @pl.when(odd)
+        def _():
+            drain(stage_late.at[:, :, 0:half_head], sends)
 
     @pl.when(y == 0)
     def _():
@@ -433,7 +517,14 @@
     def _():
         drain(kv.at[:, 0, 2:4], sends)
         drain(kv.at[0 : rows - 2, 1, 2:4], sends)
-        drain(kv.at[0, 1, 2:4, :, 0 : kv_half // 2], sends)
+
+        @pl.when(odd)
+        def _():
+            drain(kv.at[0, 1, 2:4, :, 0:half_head], sends)
+
+    @pl.when(passes)
+    def _():
+        drain(detour, sends)
 
     drain(outs.at[:, 0], sends)
     drain(norms.at[0:half], sends)
@@ -473,11 +564,11 @@
 def fused(queries, keys, values, lengths):
     rows, tok, q_width = queries.shape
     kv_width = keys.shape[2]
-    heads = lax.axis_size("heads")
+    heads, shards = lax.axis_size("heads"), lax.axis_size("dp")
     q_heads = q_width // HEAD_SIZE
     dma = pltpu.SemaphoreType.DMA
     results = pl.pallas_call(
-        functools.partial(fused_kernel, lax.axis_size("dp")),
+        functools.partial(fused_kernel, shards),
         out_shape=(
             pltpu.VMEM((rows, tok, q_width), jnp.bfloat16),
             pltpu.VMEM((q_heads // heads, rows, heads * tok), jnp.float32),
@@ -495,10 +586,12 @@
             pltpu.VMEM((rows, q_heads // 2, 2 * tok, 6 * tok), jnp.bfloat16),
             pltpu.VMEM((rows, q_heads // 2, 2 * tok, HEAD_SIZE), jnp.float32),
             pltpu.VMEM((2, tok, kv_width // 2), jnp.bfloat16),
-            pltpu.VMEM((2, tok, kv_width // 4), jnp.bfloat16),
+            pltpu.VMEM((2, tok, kv_width // 2), jnp.bfloat16),
+            pltpu.VMEM(((shards - 1) // 2, rows // 4, tok, kv_width), jnp.bfloat16),
             pltpu.VMEM(keys.shape, jnp.bfloat16),
             pltpu.VMEM(values.shape, jnp.bfloat16),
-            dma, dma, dma, dma((rows, 2)), dma((6,)), dma, dma, dma, dma((2,)), dma((2,)),
+            dma, dma, dma, dma((rows, 2)), dma((3 + rows // 2,)), dma, dma, dma, dma((2,)),
+            dma(((shards - 1) // 2,)), dma((2,)), pltpu.SemaphoreType.REGULAR,
         ],
         compiler_params=pltpu.CompilerParams(
             collective_id=0, has_side_effects=True, vmem_limit_bytes=48 * 1024 * 1024

time: 32.7 us -> 31.7 us (0.969)
  Pallas kernels: 31.9 us -> 30.9 us
    pallas_call x1, Pallas kernels: 30.9 us -> 29.9 us  [fused(): pl.pallas_call(functools.partial(fused_kernel, shards), out_shape=(pltpu....]
where the time goes in v2:
time: 31.7 us; the launch traced here: 31.5 us
  Pallas kernels  30.9 us (97%)
  between operations  0.64 us (2%)
    pallas_call x1, Pallas kernels, fused(): pl.pallas_call(functools.partial(fused_kernel, shards), out_shape=(pltpu....  29.9 us
    pallas_call x1, Pallas kernels, store(): pl.pallas_call(store_kernel, out_shape=(pltpu.HBM(attended.shape, attende...  0.99 us

profile of v2, /device:TPU:25, one launch (start us, length us, event | category | flops | bytes accessed | tf_op | source)
XLA Modules:
  0.0 31.5 jit_solution(15505043744832808585)
XLA Ops:
  0.6 29.9 %shard_map.59 = (bf16[8,64,1024]{2,1,0:T(8,128)(2,1)S(1)}, f32[2,8,256]{2,1,0:T(8,128)S(1)}) custom-call(bf16[8,64,1024]{2,1,0:T(8,128)(2,1)} %q_ref.1, bf16[8,64,512]{2,1,0:T(8,128)(2,1)} %k_ref.1, bf16[8,64,512]{2,1,0:T(8,128)(2,1)} %v_ref.1, s32[8,32]{1,0:T(8,128)} %len_ref.1), custom_call_target="tpu_custom_call" | custom-call | tf_op jit(solution)/shard_map/pallas_call | solution.py:570
  30.5 1.0 %shard_map.60 = (bf16[8,64,1024]{2,1,0:T(8,128)(2,1)}, f32[2,8,256]{2,1,0:T(8,128)}) custom-call(bf16[8,64,1024]{2,1,0:T(8,128)(2,1)S(1)} %get-tuple-element.4.out_ref, f32[2,8,256]{2,1,0:T(8,128)S(1)} %get-tuple-element.5.norm_ref), custom_call_target="tpu_custom_call" | custom-call | tf_op jit(solution)/shard_map/pallas_call | solution.py:552
